TPU v7x, 128 devices: a whole 4x4x4 slice. The times are simulated.
128 devices in a mesh: rows: 8 (over y_hi, z), bundle: 16 (over y_lo, x, core).
Axes of the slice: x: 4, y: 4 (y_hi: 2, y_lo: 2; y = y_hi * 2 + y_lo), z: 4, core: 2. Of those that a mesh axis runs over, the one named last changes fastest.
Arguments:
- raw_values: float32 [32768, 4096], P(('rows', 'bundle')), may hold values from -2100 to 2100
- bin_edges: float32 [4096, 255], P(('rows', 'bundle')), may hold values from -2100 to 2100, as said below
- feature_column: int32 [4096], replicated, may hold values from 0 to 4095, each once
- bin_offset: int32 [4096], replicated, may hold values from 0 to 63
Outputs:
- bin_codes: int32 [32768, 4096], P('rows', 'bundle')
Inputs may be any that keep to these rules, and one draw needn't show every extreme that they name: Every row of bin_edges is strictly increasing. `feature_column`: each column 0 .. 4095 is named once.
All inputs are finite; a program needn't handle non-finite values.
Results may differ from a plain program's by a relative error of at most 0.0003.
Values may be sent and summed in bfloat16 or wider, within the bound.
No kernel may reach another device: no remote copies, remote signals or barrier semaphores. Data moves between devices by JAX's collectives and lax.ppermute only.
A program may use at most 64 MiB of HBM per device.

v0:
```python
import math
import jax
import jax.numpy as jnp
from jax import lax
from jax.sharding import PartitionSpec as P


def count_below(values, edges):
    total = values.shape[0]
    block = math.gcd(total, 512)

    def one_block(part_rows):
        return jnp.sum(part_rows[:, :, None] > edges[None, :, :], axis=2, dtype=jnp.int32)

    blocks = values.reshape(total // block, block, values.shape[1])
    return lax.map(one_block, blocks).reshape(total, values.shape[1])


def local(raw_values, bin_edges, feature_column, bin_offset):
    count_feat = feature_column.shape[0]
    owner_feature = (
        jnp.zeros((count_feat,), jnp.int32)
        .at[feature_column]
        .set(jnp.arange(count_feat, dtype=jnp.int32))
    )
    edges_all = lax.all_gather(bin_edges, ("rows", "bundle"), axis=0, tiled=True)
    span_cols = count_feat // lax.axis_size("bundle")
    first_col = lax.axis_index("bundle") * span_cols
    owned_features = lax.dynamic_slice_in_dim(owner_feature, first_col, span_cols, 0)
    owned_offsets = jnp.take(bin_offset, owned_features)
    ordered = jnp.take(raw_values, owner_feature, axis=1)
    arrived = lax.all_to_all(ordered, "bundle", split_axis=1, concat_axis=0, tiled=True)
    owned_edges = jnp.take(edges_all, owned_features, axis=0)
    bins = count_below(arrived, owned_edges)
    return bins + owned_offsets[None, :]


def solution(mesh):
    in_specs = (P(("rows", "bundle"), None), P(("rows", "bundle"), None), P(), P())
    out_specs = P("rows", "bundle")
    return jax.shard_map(local, mesh=mesh, in_specs=in_specs, out_specs=out_specs, check_vma=False)
```

profile of v0, /device:TPU:1, one launch (start us, length us, event | category | flops | bytes accessed | tf_op | source)
XLA Modules:
  0.0 402.5 jit_solution(2743902135054900471)
XLA Ops:
  6.5 0.0 copy-start
  6.5 0.0 all-gather.2.cloned.1.call-start
  6.5 0.7 all-gather.2.cloned.1.call-update
  7.3 0.0 copy-start.1
  7.3 5.6 %copy.9 = f32[256,4096]{0,1:T(8,128)} copy(f32[256,4096]{1,0:T(8,128)} %param.6) | data formatting | bytes 8388608 | tf_op args[0]
  12.9 0.0 copy-done.1
  12.9 15.5 %scatter_custom_fusion = s32[4096]{0:T(1024)S(1)} fusion(s32[4096]{0:T(1024)S(1)} %compare_select_fusion.1, s32[4096]{0:T(1024)S(1)} %iota.3, s32[]{:T(128)} %copy.20), kind=kCustom, calls=%fused_computation.14 | custom fusion | bytes 16388 | tf_op jit(solution)/shard_map/scatter | solution.py:24
  28.5 18.4 %gather_fusion = f32[4096,256]{1,0:T(8,128)} fusion(f32[256,4096]{0,1:T(8,128)} %copy.9, s32[4096]{0:T(1024)S(1)} %fusion), kind=kCustom, calls=%fused_computation | custom fusion | bytes 8404992 | tf_op jit(solution)/shard_map/jit(_take)/gather | solution.py:31
  46.9 3.9 broadcast_select_fusion
  50.8 6.8 %all-to-all-start = ((f32[256,16,256]{0,2,1:T(8,128)}), f32[256,16,256]{0,2,1:T(8,128)}, u32[]{:S(2)}, u32[]{:S(2)}) async-start(f32[256,16,256]{0,2,1:T(8,128)} %broadcast_select_fusion), calls=%async_computation | async-start | bytes 8388608 | tf_op jit(solution)/shard_map/all_to_all | solution.py:32
  57.6 0.1 compare_select_fusion.2
  57.7 0.0 copy-done
  57.7 1.7 gather_fusion.2
  59.5 0.1 broadcast_select_fusion.2
  59.5 55.1 %all-to-all-done = f32[256,16,256]{0,2,1:T(8,128)} async-done(((f32[256,16,256]{0,2,1:T(8,128)}), f32[256,16,256]{0,2,1:T(8,128)}, u32[]{:S(2)}, u32[]{:S(2)}) %all-to-all-start) | async-done | bytes 4194336 | tf_op jit(solution)/shard_map/all_to_all | solution.py:32
  114.6 5.3 %copy.10 = f32[16,256,256]{2,1,0:T(8,128)} copy(f32[16,256,256]{1,2,0:T(8,128)} %bitcast.4) | data formatting | bytes 8388608 | tf_op jit(solution)/shard_map/all_to_all | solution.py:32
  119.9 122.6 %all-gather.2.cloned.1.call-done = f32[4096,255]{1,0:T(8,128)} async-done(((f32[32,255]{1,0:T(8,128)}), f32[4096,255]{1,0:T(8,128)}) %all-gather.2.cloned.1.call-update) | async-done | bytes 4177936 | tf_op jit(solution)/shard_map/all_gather | solution.py:26
  242.6 3.2 gather_fusion.1
  245.7 0.1 broadcast_select_fusion.1
  245.8 0.1 copy.11
  246.0 145.3 %while.10 = (s32[]{:T(128)}, s32[8,512,256]{2,1,0:T(8,128)}, f32[8,512,256]{2,1,0:T(8,128)}, f32[256,255]{0,1:T(8,128)S(1)}, s32[]{:T(128)}) while((s32[]{:T(128)}, s32[8,512,256]{2,1,0:T(8,128)}, f32[8,512,256]{2,1,0:T(8,128)}, f32[256,255]{0,1:T(8,128)S(1)}, s32[]{:T(128)}) %tuple.25), condition=%wide.region_3.4_spmd, body=%wide.region_1.0_spmd.sunk | while | flops 100139008 | bytes 3407425 | solution.py:16
  246.0 1.1 dynamic-slice_bitcast_fusion.2
  247.1 16.2 %convert_reduce_fusion.2 = s32[512,256]{1,0:T(8,128)S(1)} fusion(f32[256,255]{0,1:T(8,128)S(1)} %get-tuple-element.80, f32[512,256]{1,0:T(8,128)S(1)} %dynamic-slice_bitcast_fusion.2), kind=kLoop, calls=%fused_computation.4.clone.1 | loop fusion | flops 100139008 | bytes 1309696 | tf_op jit(solution)/shard_map/while/body/eval_jaxpr/reduce_sum | solution.py:13
  263.3 0.9 bitcast_dynamic-update-slice_fusion.2
  264.1 1.1 dynamic-slice_bitcast_fusion.2
  265.2 16.2 %convert_reduce_fusion.2 = s32[512,256]{1,0:T(8,128)S(1)} fusion(f32[256,255]{0,1:T(8,128)S(1)} %get-tuple-element.80, f32[512,256]{1,0:T(8,128)S(1)} %dynamic-slice_bitcast_fusion.2), kind=kLoop, calls=%fused_computation.4.clone.1 | loop fusion | flops 100139008 | bytes 1309696 | tf_op jit(solution)/shard_map/while/body/eval_jaxpr/reduce_sum | solution.py:13
  281.4 0.9 bitcast_dynamic-update-slice_fusion.2
  282.3 1.1 dynamic-slice_bitcast_fusion.2
  283.4 16.2 %convert_reduce_fusion.2 = s32[512,256]{1,0:T(8,128)S(1)} fusion(f32[256,255]{0,1:T(8,128)S(1)} %get-tuple-element.80, f32[512,256]{1,0:T(8,128)S(1)} %dynamic-slice_bitcast_fusion.2), kind=kLoop, calls=%fused_computation.4.clone.1 | loop fusion | flops 100139008 | bytes 1309696 | tf_op jit(solution)/shard_map/while/body/eval_jaxpr/reduce_sum | solution.py:13
  299.6 0.9 bitcast_dynamic-update-slice_fusion.2
  300.5 1.1 dynamic-slice_bitcast_fusion.2
  301.5 16.2 %convert_reduce_fusion.2 = s32[512,256]{1,0:T(8,128)S(1)} fusion(f32[256,255]{0,1:T(8,128)S(1)} %get-tuple-element.80, f32[512,256]{1,0:T(8,128)S(1)} %dynamic-slice_bitcast_fusion.2), kind=kLoop, calls=%fused_computation.4.clone.1 | loop fusion | flops 100139008 | bytes 1309696 | tf_op jit(solution)/shard_map/while/body/eval_jaxpr/reduce_sum | solution.py:13
  317.8 0.8 bitcast_dynamic-update-slice_fusion.2
  318.6 1.1 dynamic-slice_bitcast_fusion.2
  319.7 16.2 %convert_reduce_fusion.2 = s32[512,256]{1,0:T(8,128)S(1)} fusion(f32[256,255]{0,1:T(8,128)S(1)} %get-tuple-element.80, f32[512,256]{1,0:T(8,128)S(1)} %dynamic-slice_bitcast_fusion.2), kind=kLoop, calls=%fused_computation.4.clone.1 | loop fusion | flops 100139008 | bytes 1309696 | tf_op jit(solution)/shard_map/while/body/eval_jaxpr/reduce_sum | solution.py:13
  335.9 0.9 bitcast_dynamic-update-slice_fusion.2
  336.8 1.1 dynamic-slice_bitcast_fusion.2
  337.8 16.2 %convert_reduce_fusion.2 = s32[512,256]{1,0:T(8,128)S(1)} fusion(f32[256,255]{0,1:T(8,128)S(1)} %get-tuple-element.80, f32[512,256]{1,0:T(8,128)S(1)} %dynamic-slice_bitcast_fusion.2), kind=kLoop, calls=%fused_computation.4.clone.1 | loop fusion | flops 100139008 | bytes 1309696 | tf_op jit(solution)/shard_map/while/body/eval_jaxpr/reduce_sum | solution.py:13
  354.1 0.8 bitcast_dynamic-update-slice_fusion.2
  354.9 1.1 dynamic-slice_bitcast_fusion.2
  356.0 16.2 %convert_reduce_fusion.2 = s32[512,256]{1,0:T(8,128)S(1)} fusion(f32[256,255]{0,1:T(8,128)S(1)} %get-tuple-element.80, f32[512,256]{1,0:T(8,128)S(1)} %dynamic-slice_bitcast_fusion.2), kind=kLoop, calls=%fused_computation.4.clone.1 | loop fusion | flops 100139008 | bytes 1309696 | tf_op jit(solution)/shard_map/while/body/eval_jaxpr/reduce_sum | solution.py:13
  372.2 0.8 bitcast_dynamic-update-slice_fusion.2
  373.0 1.1 dynamic-slice_bitcast_fusion.2
  374.1 16.2 %convert_reduce_fusion.2 = s32[512,256]{1,0:T(8,128)S(1)} fusion(f32[256,255]{0,1:T(8,128)S(1)} %get-tuple-element.80, f32[512,256]{1,0:T(8,128)S(1)} %dynamic-slice_bitcast_fusion.2), kind=kLoop, calls=%fused_computation.4.clone.1 | loop fusion | flops 100139008 | bytes 1309696 | tf_op jit(solution)/shard_map/while/body/eval_jaxpr/reduce_sum | solution.py:13
  390.3 0.9 bitcast_dynamic-update-slice_fusion.2
  391.2 4.5 %bitcast_add_fusion = s32[4096,256]{1,0:T(8,128)} fusion(s32[8,512,256]{2,1,0:T(8,128)} %get-tuple-element.27, s32[256]{0:T(256)S(1)} %get-tuple-element.40), kind=kLoop, calls=%fused_computation.7 | loop fusion | flops 1048576 | bytes 8389632 | tf_op jit(solution)/shard_map/add | solution.py:35
  (7 shorter events, 0.0 us)
Async XLA Ops:
  6.5 51.2 %copy-start = (s32[4096]{0:T(1024)S(1)}, s32[4096]{0:T(1024)}, u32[]{:S(2)}) copy-start(s32[4096]{0:T(1024)} %param.9) | copy-start | bytes 49156
  6.5 236.0 %all-gather.2.cloned.1.call-start = ((), (), s32[]{:S(2)}) async-start(), calls=%async_computation.1 | async-start | bytes 4227072 | tf_op jit(solution)/shard_map/all_gather | solution.py:26
  7.3 5.6 %copy-start.1 = (s32[4096]{0:T(1024)S(1)}, s32[4096]{0:T(1024)}, u32[]{:S(2)}) copy-start(s32[4096]{0:T(1024)} %param.8) | copy-start | bytes 49156
  50.8 63.8 %all-to-all-start = ((f32[256,16,256]{0,2,1:T(8,128)}), f32[256,16,256]{0,2,1:T(8,128)}, u32[]{:S(2)}, u32[]{:S(2)}) async-start(f32[256,16,256]{0,2,1:T(8,128)} %broadcast_select_fusion), calls=%async_computation | async-start | bytes 8388608 | tf_op jit(solution)/shard_map/all_to_all | solution.py:32
Sparse Core Ops, SparseCore 0:
  9.1 233.4 all-gather.1
where the time goes:
time: 403 us
  waiting for transfers between devices  178 us (44%)
  other arithmetic  139 us (34%)
  local copies, waits for them, and re-layouts  65.2 us (16%)
  between operations  13.5 us (3%)
  starting transfers between devices  6.83 us (2%)
    reduce_sum x8, other arithmetic, one_block(): jnp.sum(part_rows[:, :, None] > edges[None, :, :], axis=2, dtype=jnp.int32)  130 us
    all_gather x1, waiting for transfers between devices, local(): lax.all_gather(bin_edges, ('rows', 'bundle'), axis=0, tiled=True)  123 us
    all_to_all x1, waiting for transfers between devices, local(): lax.all_to_all(ordered, 'bundle', split_axis=1, concat_axis=0, tiled=True)  55.1 us
    gather x1, local copies, waits for them, and re-layouts, local(): ordered = jnp.take(raw_values, owner_feature, axis=1)  18.4 us
    scatter x1, local copies, waits for them, and re-layouts, local(): owner_feature = jnp.zeros((count_feat,), jnp.int32).at[feature_column].se...  15.5 us
    gt x8, local copies, waits for them, and re-layouts, one_block(): part_rows[:, :, None] > edges[None, :, :]  8.61 us
  transfers between devices with their start and end apart: 2, of which 2 were waited for; matrix products, arithmetic and copies ran while one was open for 13% of the time, Pallas kernels for 0%

commit v1 on v0

--- a/solution.py
+++ b/solution.py
@@ -23,7 +23,16 @@
         .at[feature_column]
         .set(jnp.arange(count_feat, dtype=jnp.int32))
     )
-    edges_all = lax.all_gather(bin_edges, ("rows", "bundle"), axis=0, tiled=True)
+    settle_the_pages = lambda shard_axis, w_in: jnp.concatenate(
+        lax.all_to_all(
+            jnp.stack([w_in for _ in range(lax.axis_size(shard_axis))], axis=0),
+            split_axis=0,
+            axis_name=shard_axis,
+            concat_axis=0,
+        ),
+        axis=0,
+    )
+    edges_all = settle_the_pages(("rows", "bundle"), bin_edges)
     span_cols = count_feat // lax.axis_size("bundle")
     first_col = lax.axis_index("bundle") * span_cols
     owned_features = lax.dynamic_slice_in_dim(owner_feature, first_col, span_cols, 0)

time: 403 us -> 317 us (0.79)
  waiting for transfers between devices: 178 us -> 45.1 us
  blocking collectives: 0 us -> 55.5 us
  between operations: 13.5 us -> 0.1 us
    all_gather x1 -> x0, waiting for transfers between devices: 123 us -> none  [local(): lax.all_gather(bin_edges, ('rows', 'bundle'), axis=0, tiled=True)]
    all_to_all x0 -> x1, blocking collectives: none -> 55.5 us  [local(): lax.all_to_all(ordered, 'bundle', split_axis=1, concat_axis=0, tiled=True)]
    all_to_all x1, waiting for transfers between devices: 55.1 us -> 45.1 us  [local(): lax.all_to_all(jnp.stack([w_in for _ in range(lax.axis_size(shard_axis))]...]
  transfers between devices with their start and end apart: 2 -> 1, of which waited for: 2 -> 1; matrix products, arithmetic and copies ran while one was open for 13% -> 2% of each run, Pallas kernels for 0% -> 0%
where the time goes in v1:
time: 317 us; the launch traced here: 316 us
  other arithmetic  139 us (44%)
  local copies, waits for them, and re-layouts  67.5 us (21%)
  blocking collectives  55.5 us (18%)
  waiting for transfers between devices  45.1 us (14%)
  starting transfers between devices  9.13 us (3%)
    reduce_sum x8, other arithmetic, one_block(): jnp.sum(part_rows[:, :, None] > edges[None, :, :], axis=2, dtype=jnp.int32)  130 us
    all_to_all x1, blocking collectives, local(): lax.all_to_all(ordered, 'bundle', split_axis=1, concat_axis=0, tiled=True)  55.5 us
    all_to_all x1, waiting for transfers between devices, local(): lax.all_to_all(jnp.stack([w_in for _ in range(lax.axis_size(shard_axis))]...  45.1 us
    gather x1, local copies, waits for them, and re-layouts, local(): ordered = jnp.take(raw_values, owner_feature, axis=1)  18.3 us
    scatter x1, local copies, waits for them, and re-layouts, local(): owner_feature = jnp.zeros((count_feat,), jnp.int32).at[feature_column].se...  15.5 us
    all_to_all x1, starting transfers between devices, local(): lax.all_to_all(jnp.stack([w_in for _ in range(lax.axis_size(shard_axis))]...  9.13 us
    gt x8, local copies, waits for them, and re-layouts, one_block(): part_rows[:, :, None] > edges[None, :, :]  8.61 us
    dynamic_update_slice x8, local copies, waits for them, and re-layouts, count_below(): return lax.map(one_block, blocks).reshape(total, values.shape[1])  6.68 us
  transfers between devices with their start and end apart: 1, of which 1 were waited for; matrix products, arithmetic and copies ran while one was open for 2% of the time, Pallas kernels for 0%

profile of v1, /device:TPU:1, one launch (start us, length us, event | category | flops | bytes accessed | tf_op | source)
XLA Modules:
  0.0 316.0 jit_solution(4781758298036527332)
XLA Ops:
  0.0 0.0 copy-start
  0.0 0.7 compare_select_fusion.1
  0.7 15.5 %scatter_custom_fusion = s32[4096]{0:T(1024)S(1)} fusion(s32[4096]{0:T(1024)S(1)} %compare_select_fusion.1, s32[4096]{0:T(1024)S(1)} %iota.3, s32[]{:T(128)} %copy.20), kind=kCustom, calls=%fused_computation.14 | custom fusion | bytes 16388 | tf_op jit(solution)/shard_map/scatter | solution.py:24
  16.3 5.6 %copy.9 = f32[256,4096]{0,1:T(8,128)} copy(f32[256,4096]{1,0:T(8,128)} %param.6) | data formatting | bytes 8388608 | tf_op args[0]
  21.9 18.3 %gather_fusion = f32[4096,256]{1,0:T(8,128)} fusion(f32[256,4096]{0,1:T(8,128)} %copy.9, s32[4096]{0:T(1024)S(1)} %fusion), kind=kCustom, calls=%fused_computation | custom fusion | bytes 8404992 | tf_op jit(solution)/shard_map/jit(_take)/gather | solution.py:40
  40.2 3.3 %broadcast_select_fusion = f32[256,16,256]{0,2,1:T(8,128)S(1)} fusion(f32[256,16,256]{0,2,1:T(8,128)} %bitcast.16, pred[16,256]{1,0:T(8,128)(4,1)S(1)} %broadcast_in_dim.47), kind=kLoop, calls=%fused_computation.8 | loop fusion | flops 1048576 | bytes 8392704 | tf_op jit(solution)/shard_map/jit(_take)/select_n | solution.py:40
  43.5 0.0 copy-start.1
  43.5 55.5 %all_to_all.18 = f32[256,16,256]{0,2,1:T(8,128)} all-to-all(f32[256,16,256]{0,2,1:T(8,128)S(1)} %broadcast_select_fusion), channel_id=1, replica_groups=mesh['rows'=8,'bundle'=16] {'bundle'}, dimensions={1} | all-to-all | bytes 8388608 | tf_op jit(solution)/shard_map/all_to_all | solution.py:41
  99.0 0.0 copy-done.1
  99.0 2.5 stack.2
  101.5 9.1 %all-to-all-start.1 = ((f32[128,32,255]{2,1,0:T(8,128)}), f32[128,32,255]{2,1,0:T(8,128)}, u32[]{:S(2)}, u32[]{:S(2)}) async-start(f32[128,32,255]{2,1,0:T(8,128)} %stack.2), calls=%async_computation.1 | async-start | bytes 8388608 | tf_op jit(solution)/shard_map/all_to_all | solution.py:27
  110.6 0.1 compare_select_fusion.2
  110.7 0.0 copy-done
  110.7 1.7 gather_fusion.2
  112.5 0.1 broadcast_select_fusion.2
  112.5 5.3 %copy.10 = f32[16,256,256]{2,1,0:T(8,128)} copy(f32[16,256,256]{1,2,0:T(8,128)} %bitcast.17) | data formatting | bytes 8388608 | tf_op jit(solution)/shard_map/all_to_all | solution.py:41
  117.9 45.1 %all-to-all-done.1 = f32[128,32,255]{2,1,0:T(8,128)} async-done(((f32[128,32,255]{2,1,0:T(8,128)}), f32[128,32,255]{2,1,0:T(8,128)}, u32[]{:S(2)}, u32[]{:S(2)}) %all-to-all-start.1) | async-done | bytes 4177952 | tf_op jit(solution)/shard_map/all_to_all | solution.py:27
  163.0 3.2 gather_fusion.1
  166.2 0.1 broadcast_select_fusion.1
  166.3 0.1 copy.11
  166.4 145.1 %while.10 = (s32[]{:T(128)}, s32[8,512,256]{2,1,0:T(8,128)}, f32[8,512,256]{2,1,0:T(8,128)}, f32[256,255]{0,1:T(8,128)S(1)}, s32[]{:T(128)}) while((s32[]{:T(128)}, s32[8,512,256]{2,1,0:T(8,128)}, f32[8,512,256]{2,1,0:T(8,128)}, f32[256,255]{0,1:T(8,128)S(1)}, s32[]{:T(128)}) %tuple.23), condition=%wide.region_3.4_spmd, body=%wide.region_1.0_spmd.sunk | while | flops 100139008 | bytes 3407425 | solution.py:16
  166.4 1.1 dynamic-slice_bitcast_fusion.2
  167.5 16.2 %convert_reduce_fusion.2 = s32[512,256]{1,0:T(8,128)S(1)} fusion(f32[256,255]{0,1:T(8,128)S(1)} %get-tuple-element.80, f32[512,256]{1,0:T(8,128)S(1)} %dynamic-slice_bitcast_fusion.2), kind=kLoop, calls=%fused_computation.4.clone.1 | loop fusion | flops 100139008 | bytes 1309696 | tf_op jit(solution)/shard_map/while/body/eval_jaxpr/reduce_sum | solution.py:13
  183.7 0.8 bitcast_dynamic-update-slice_fusion.2
  184.6 1.1 dynamic-slice_bitcast_fusion.2
  185.6 16.2 %convert_reduce_fusion.2 = s32[512,256]{1,0:T(8,128)S(1)} fusion(f32[256,255]{0,1:T(8,128)S(1)} %get-tuple-element.80, f32[512,256]{1,0:T(8,128)S(1)} %dynamic-slice_bitcast_fusion.2), kind=kLoop, calls=%fused_computation.4.clone.1 | loop fusion | flops 100139008 | bytes 1309696 | tf_op jit(solution)/shard_map/while/body/eval_jaxpr/reduce_sum | solution.py:13
  201.9 0.8 bitcast_dynamic-update-slice_fusion.2
  202.7 1.1 dynamic-slice_bitcast_fusion.2
  203.8 16.2 %convert_reduce_fusion.2 = s32[512,256]{1,0:T(8,128)S(1)} fusion(f32[256,255]{0,1:T(8,128)S(1)} %get-tuple-element.80, f32[512,256]{1,0:T(8,128)S(1)} %dynamic-slice_bitcast_fusion.2), kind=kLoop, calls=%fused_computation.4.clone.1 | loop fusion | flops 100139008 | bytes 1309696 | tf_op jit(solution)/shard_map/while/body/eval_jaxpr/reduce_sum | solution.py:13
  220.0 0.8 bitcast_dynamic-update-slice_fusion.2
  220.8 1.1 dynamic-slice_bitcast_fusion.2
  221.9 16.2 %convert_reduce_fusion.2 = s32[512,256]{1,0:T(8,128)S(1)} fusion(f32[256,255]{0,1:T(8,128)S(1)} %get-tuple-element.80, f32[512,256]{1,0:T(8,128)S(1)} %dynamic-slice_bitcast_fusion.2), kind=kLoop, calls=%fused_computation.4.clone.1 | loop fusion | flops 100139008 | bytes 1309696 | tf_op jit(solution)/shard_map/while/body/eval_jaxpr/reduce_sum | solution.py:13
  238.1 0.8 bitcast_dynamic-update-slice_fusion.2
  239.0 1.1 dynamic-slice_bitcast_fusion.2
  240.1 16.2 %convert_reduce_fusion.2 = s32[512,256]{1,0:T(8,128)S(1)} fusion(f32[256,255]{0,1:T(8,128)S(1)} %get-tuple-element.80, f32[512,256]{1,0:T(8,128)S(1)} %dynamic-slice_bitcast_fusion.2), kind=kLoop, calls=%fused_computation.4.clone.1 | loop fusion | flops 100139008 | bytes 1309696 | tf_op jit(solution)/shard_map/while/body/eval_jaxpr/reduce_sum | solution.py:13
  256.3 0.8 bitcast_dynamic-update-slice_fusion.2
  257.1 1.1 dynamic-slice_bitcast_fusion.2
  258.2 16.2 %convert_reduce_fusion.2 = s32[512,256]{1,0:T(8,128)S(1)} fusion(f32[256,255]{0,1:T(8,128)S(1)} %get-tuple-element.80, f32[512,256]{1,0:T(8,128)S(1)} %dynamic-slice_bitcast_fusion.2), kind=kLoop, calls=%fused_computation.4.clone.1 | loop fusion | flops 100139008 | bytes 1309696 | tf_op jit(solution)/shard_map/while/body/eval_jaxpr/reduce_sum | solution.py:13
  274.4 0.8 bitcast_dynamic-update-slice_fusion.2
  275.3 1.1 dynamic-slice_bitcast_fusion.2
  276.3 16.2 %convert_reduce_fusion.2 = s32[512,256]{1,0:T(8,128)S(1)} fusion(f32[256,255]{0,1:T(8,128)S(1)} %get-tuple-element.80, f32[512,256]{1,0:T(8,128)S(1)} %dynamic-slice_bitcast_fusion.2), kind=kLoop, calls=%fused_computation.4.clone.1 | loop fusion | flops 100139008 | bytes 1309696 | tf_op jit(solution)/shard_map/while/body/eval_jaxpr/reduce_sum | solution.py:13
  292.6 0.8 bitcast_dynamic-update-slice_fusion.2
  293.4 1.1 dynamic-slice_bitcast_fusion.2
  294.5 16.2 %convert_reduce_fusion.2 = s32[512,256]{1,0:T(8,128)S(1)} fusion(f32[256,255]{0,1:T(8,128)S(1)} %get-tuple-element.80, f32[512,256]{1,0:T(8,128)S(1)} %dynamic-slice_bitcast_fusion.2), kind=kLoop, calls=%fused_computation.4.clone.1 | loop fusion | flops 100139008 | bytes 1309696 | tf_op jit(solution)/shard_map/while/body/eval_jaxpr/reduce_sum | solution.py:13
  310.7 0.8 bitcast_dynamic-update-slice_fusion.2
  311.5 4.5 %bitcast_add_fusion = s32[4096,256]{1,0:T(8,128)} fusion(s32[8,512,256]{2,1,0:T(8,128)} %get-tuple-element.27, s32[256]{0:T(256)S(1)} %get-tuple-element.40), kind=kLoop, calls=%fused_computation.7 | loop fusion | flops 1048576 | bytes 8389632 | tf_op jit(solution)/shard_map/add | solution.py:44
  (6 shorter events, 0.0 us)
Async XLA Ops:
  0.0 110.7 %copy-start = (s32[4096]{0:T(1024)S(1)}, s32[4096]{0:T(1024)}, u32[]{:S(2)}) copy-start(s32[4096]{0:T(1024)} %param.9) | copy-start | bytes 49156
  43.5 55.5 %copy-start.1 = (f32[32,255]{1,0:T(8,128)S(1)}, f32[32,255]{1,0:T(8,128)}, u32[]{:S(2)}) copy-start(f32[32,255]{1,0:T(8,128)} %param.7) | copy-start | bytes 97924
  101.5 61.5 %all-to-all-start.1 = ((f32[128,32,255]{2,1,0:T(8,128)}), f32[128,32,255]{2,1,0:T(8,128)}, u32[]{:S(2)}, u32[]{:S(2)}) async-start(f32[128,32,255]{2,1,0:T(8,128)} %stack.2), calls=%async_computation.1 | async-start | bytes 8388608 | tf_op jit(solution)/shard_map/all_to_all | solution.py:27
